TPU v7x, 32 devices: a whole 2x2x4 slice. The times are simulated.
32 devices in a mesh: chain: 8 (over y, x, core), par: 4 (over z).
Axes of the slice: x: 2, y: 2, z: 4, core: 2. Of those that a mesh axis runs over, the one named last changes fastest.
Arguments:
- propagation_gains: bfloat16 [4, 16, 64, 8192], P('par', None, None, 'chain'), may hold values from -0.13258252 to 0.13258252, as said below
- observed_samples: bfloat16 [4, 16, 32, 8192], P('par', None, None, 'chain'), may hold values from -6 to 6
- disturbance_variance: float32 [4, 16], P(None, 'chain'), may hold values from 0.05 to 0.5
- retained_branches: int32 [4, 16, 16, 1024], P(None, 'chain', 'par'), may hold values from 0 to 63
Outputs:
- distances: float32 [4, 16, 16, 1024], P(None, 'chain', 'par')
Inputs may be any that keep to these rules, and one draw needn't show every extreme that they name: `propagation_gains`: row 2u holds the real and row 2u+1 the imaginary part of the channel to user u.
All inputs are finite; a program needn't handle non-finite values.
Results may differ from a plain program's by a relative error of at most 0.0003.
Values sent between devices are 32-bit elements; how exact they have to be, the bound alone decides.
A program may use at most 64 MiB of HBM per device.

v0:
```python
import jax
import jax.numpy as jnp
from jax import lax
from jax.sharding import PartitionSpec as P

constellation_norm = 1.0 / 42.0**0.5


def prefix(x, axis, combine, identity):
    length, here = (lax.axis_size(axis), lax.axis_index(axis))
    everything = jax.tree.map(lambda part: lax.all_gather(part, axis), x)
    start = jax.tree.map(
        lambda part, zero: jnp.broadcast_to(jnp.asarray(zero, part.dtype), part.shape), x, identity
    )

    def turn(k, before):
        reached = k < here
        new = combine(before, jax.tree.map(lambda part: part[k], everything))
        return jax.tree.map(lambda a, b: jnp.where(reached, a, b), new, before)

    return lax.fori_loop(0, length, turn, start)


def from_root(block, axis, owner):
    block = jnp.where(lax.axis_index(axis) == owner, block, jnp.zeros_like(block))
    return lax.psum(block, axis)


def fold_stats(raw_gram, raw_cross):
    outer_dimensions = raw_gram.shape[:-2]
    terminal_number = raw_gram.shape[-1] // 2
    pieces = raw_gram.reshape(outer_dimensions + (terminal_number, 2, terminal_number, 2))
    same_part = pieces[..., :, 0, :, 0] + pieces[..., :, 1, :, 1]
    cross_part = pieces[..., :, 1, :, 0] - pieces[..., :, 0, :, 1]
    crossed = raw_cross.reshape(outer_dimensions + (terminal_number, 2, -1, 2))
    rhs_real = crossed[..., :, 0, :, 0] + crossed[..., :, 1, :, 1]
    rhs_imag = crossed[..., :, 0, :, 1] - crossed[..., :, 1, :, 0]
    rhs = jnp.stack([rhs_real, rhs_imag], axis=-2).reshape(
        outer_dimensions + (2 * terminal_number, -1)
    )
    return (same_part, cross_part, rhs)


def assemble(same_part, cross_part, noise):
    row_even = jnp.stack([same_part, cross_part], axis=-1)
    row_odd = jnp.stack([-cross_part, same_part], axis=-1)
    whole = jnp.stack([row_even, row_odd], axis=-3)
    order = 2 * same_part.shape[-1]
    gram = whole.reshape(same_part.shape[:-2] + (order, order))
    return gram + noise[..., None, None] * jnp.eye(order, dtype=jnp.float32)


def estimate_transmitted(cholesky_triangle, whitened_observation, retained_branches):
    terminal_number = cholesky_triangle.shape[-1] // 2
    outer_dimensions = retained_branches.shape[:-1]
    kept_branch_number = retained_branches.shape[-1] // terminal_number
    constellation_position = retained_branches.reshape(
        outer_dimensions + (kept_branch_number, terminal_number)
    )
    inphase_amplitude = (2 * (constellation_position % 8) - 7).astype(jnp.float32)
    quadrature_amplitude = (2 * (constellation_position // 8) - 7).astype(jnp.float32)
    branch_vector = (
        jnp.stack([inphase_amplitude, quadrature_amplitude], axis=-1).reshape(
            outer_dimensions + (kept_branch_number, 2 * terminal_number)
        )
        * constellation_norm
    )
    upper_factor = jnp.swapaxes(cholesky_triangle, -1, -2)
    mapped = jnp.einsum(
        "bsij,bstkj->bstki", upper_factor, branch_vector, precision=lax.Precision.HIGHEST
    )
    remainder_error = jnp.swapaxes(whitened_observation, -1, -2)[..., None, :] - mapped
    squared_errors = (
        (remainder_error * remainder_error)
        .reshape(outer_dimensions + (kept_branch_number, terminal_number, 2))
        .sum(axis=-1)
    )
    accrued_metric = jnp.cumsum(squared_errors[..., ::-1], axis=-1)[..., ::-1] / terminal_number
    return accrued_metric.reshape(outer_dimensions + (kept_branch_number * terminal_number,))


def add_tree(earlier, later):
    return jax.tree.map(jnp.add, earlier, later)


def flatten_last(array_in):
    return array_in.reshape(array_in.shape[:2] + (-1,))


def local(propagation_gains, observed_samples, disturbance_variance, retained_branches):
    terminal_number = propagation_gains.shape[2] // 2
    sym_total = observed_samples.shape[2] // 2
    clusters = lax.axis_size("chain")
    sub_share = propagation_gains.shape[1] // clusters
    raw_gram = jnp.einsum(
        "bsra,bsqa->bsrq", propagation_gains, propagation_gains, preferred_element_type=jnp.float32
    )
    raw_cross = jnp.einsum(
        "bsra,bsqa->bsrq", propagation_gains, observed_samples, preferred_element_type=jnp.float32
    )
    statistic = (flatten_last(raw_gram), flatten_last(raw_cross))
    zeros_tree = jax.tree.map(jnp.zeros_like, statistic)
    earlier = prefix(statistic, "chain", add_tree, zeros_tree)
    running = add_tree(earlier, statistic)
    totals = jax.tree.map(lambda part: from_root(part, "chain", clusters - 1), running)
    start = lax.axis_index("chain") * sub_share
    shares = jax.tree.map(
        lambda whole: lax.dynamic_slice_in_dim(whole, start, sub_share, 1), totals
    )
    outer_dimensions = (1, sub_share)
    same_part, cross_part, rhs = fold_stats(
        shares[0].reshape(outer_dimensions + (2 * terminal_number, 2 * terminal_number)),
        shares[1].reshape(outer_dimensions + (2 * terminal_number, 2 * sym_total)),
    )
    band_index = lax.axis_index("par")
    own_noise = lax.dynamic_slice_in_dim(disturbance_variance, band_index, 1, 0)
    lower_own = jnp.linalg.cholesky(assemble(same_part, cross_part, own_noise))
    rotated_own = jax.scipy.linalg.solve_triangular(lower_own, rhs, lower=True)
    cholesky_triangle = lax.all_gather(lower_own, "par", axis=0, tiled=True)
    whitened_observation = lax.all_to_all(
        rotated_own, "par", split_axis=3, concat_axis=0, tiled=True
    )
    return estimate_transmitted(cholesky_triangle, whitened_observation, retained_branches)


def solution(mesh):
    placed = (
        P("par", None, None, "chain"),
        P("par", None, None, "chain"),
        P(None, "chain"),
        P(None, "chain", "par", None),
    )
    return jax.shard_map(
        local, mesh=mesh, in_specs=placed, out_specs=P(None, "chain", "par", None), check_vma=False
    )
```

profile of v0, /device:TPU:0, one launch (start us, length us, event | category | flops | bytes accessed | tf_op | source)
XLA Modules:
  0.0 226.0 jit_solution(8765339987140583563)
XLA Ops:
  6.5 1.6 copy-done
  8.1 1.9 fusion
  10.0 0.9 all_gather_reshape.7
  11.7 0.9 all_gather_reshape.6
  12.7 0.9 reshape.316
  15.1 1.1 reshape.317
  17.0 1.3 copy.136
  18.5 18.7 %all-gather.5.cloned.1.call-done = f32[8,1,16,2048]{3,2,1,0:T(8,128)} async-done(((f32[1,1,16,2048]{3,2,1,0:T(8,128)}), f32[8,1,16,2048]{3,2,1,0:T(8,128)}) %all-gather.5.cloned.1.call-update) | async-done | bytes 1048592 | tf_op jit(solution)/shard_map/all_gather | solution.py:11
  37.2 29.7 %all-gather.3.cloned.1.call-done = f32[8,1,16,4096]{3,2,1,0:T(8,128)} async-done(((f32[1,1,16,4096]{3,2,1,0:T(8,128)}), f32[8,1,16,4096]{3,2,1,0:T(8,128)}) %all-gather.3.cloned.1.call-update) | async-done | bytes 2097168 | tf_op jit(solution)/shard_map/all_gather | solution.py:11
  66.9 16.1 %while.16 = (s32[]{:T(128)}, f32[1,16,4096]{2,1,0:T(8,128)S(1)}, f32[1,16,2048]{2,1,0:T(8,128)S(1)}, s32[]{:T(128)}, f32[8,1,16,4096]{3,2,1,0:T(8,128)}, /*index=5*/f32[8,1,16,2048]{3,2,1,0:T(8,128)}, s32[]{:T(128)}, s32[]{:T(128)}) while((s32[]{:T(128)}, f32[1,16,4096]{2,1,0:T(8,128)S(1)}, f32[1,16,2048]{2,1,0:T(8,128)S(1)}, ...), condition=%wide.region_1.2_spmd.clone, body=%wide.region_0.1_spmd.clone.sunk | while | flops 294916 | bytes 1179771 | solution.py:21
  66.9 1.0 add_select_fusion.9
  67.9 1.0 add_select_fusion.8
  69.0 0.9 add_select_fusion.9
  69.9 1.0 add_select_fusion.8
  71.0 0.9 add_select_fusion.9
  71.9 1.0 add_select_fusion.8
  73.0 0.9 add_select_fusion.9
  73.9 1.0 add_select_fusion.8
  75.0 0.9 add_select_fusion.9
  76.0 1.0 add_select_fusion.8
  77.0 0.9 add_select_fusion.9
  78.0 1.0 add_select_fusion.8
  79.0 0.9 add_select_fusion.9
  80.0 1.0 add_select_fusion.8
  81.0 0.9 add_select_fusion.9
  82.0 1.0 add_select_fusion.8
  84.5 54.6 %all-reduce.3.cloned.1.call-done = (f32[1,16,4096]{2,1,0:T(8,128)}, f32[1,16,2048]{2,1,0:T(8,128)}) async-done(((f32[1,16,4096]{2,1,0:T(8,128)}, f32[1,16,2048]{2,1,0:T(8,128)}), (f32[1,16,4096]{2,1,0:T(8,128)}, f32[1,16,2048]{2,1,0:T(8,128)})) %all-reduce.3.cloned.1.call-update) | async-done | bytes 393232 | tf_op jit(solution)/shard_map/psum | solution.py:26
  139.2 0.9 constant_dynamic-slice_fusion.1
  140.9 1.0 reshape_reshape.7
  141.9 1.3 slice_add_fusion.1
  143.3 1.3 copy.129
  144.6 1.3 copy.130
  146.0 3.5 %reshape_reshape.6 = f32[1,2,32,2,32,2]{5,4,3,2,1,0:T(8,128)} reshape(f32[1,2,4096]{2,1,0:T(2,128)S(1)} %constant_dynamic-slice_fusion.1) | data formatting | bytes 65536 | tf_op jit(solution)/shard_map/reshape;reshape | solution.py:32
  149.5 3.4 %fusion.5 = (f32[2,32,32]{2,1,0:T(8,128)S(1)}, f32[2,32,32]{2,1,0:T(8,128)S(1)}) fusion(f32[1,2,32,2,32,2]{5,4,3,2,1,0:T(8,128)} %reshape_reshape.6), kind=kLoop, calls=%fused_computation.10 | loop fusion | flops 4096 | bytes 49152 | tf_op jit(solution)/shard_map/sub | solution.py:34
  153.0 3.0 %copy.146 = f32[1,2,32,2,32,2]{3,2,5,4,1,0:T(8,128)} copy(f32[1,2,32,2,32,2]{4,2,1,5,3,0:T(8,128)S(1)} %pad_maximum_fusion) | data formatting | bytes 65536 | tf_op jit(solution)/shard_map/reshape | solution.py:49
  156.0 3.3 %reshape.321 = f32[1,2,64,64]{2,3,1,0:T(8,128)S(1)} reshape(f32[1,2,32,2,32,2]{3,2,5,4,1,0:T(8,128)} %copy.146) | data formatting | bytes 65536 | tf_op jit(solution)/shard_map/reshape | solution.py:49
  159.5 11.7 %custom-call.8 = f32[1,2,64,64]{3,2,1,0:T(8,128)S(1)} custom-call(f32[1,2,64,64]{3,2,1,0:T(8,128)S(1)} %fusion.18), custom_call_target="Cholesky" | custom-call | tf_op jit(solution)/shard_map/jit(cholesky)/cholesky | solution.py:117
  171.5 9.8 %custom-call.9 = f32[2,1,64,64]{2,3,1,0:T(8,128)S(1)} custom-call(f32[2,1,64,64]{3,2,1,0:T(8,128)S(1)} %get-tuple-element.154), custom_call_target="InvertDiagBlocksLowerTriangular" | custom-call | tf_op jit(solution)/shard_map/jit(_solve_triangular)/vmap()/triangular_solve | solution.py:118
  182.3 4.5 %all-to-all-start = ((f32[4,1,512]{2,1,0:T(1,128)}), f32[4,1,512]{2,1,0:T(1,128)S(1)}, u32[]{:S(2)}, u32[]{:S(2)}) async-start(f32[4,1,512]{2,1,0:T(1,128)} %reshape.325), calls=%async_computation | async-start | bytes 16384 | tf_op jit(solution)/shard_map/all_to_all | solution.py:120
  186.8 14.5 %all_gather.11 = f32[4,2,64,64]{3,2,1,0:T(8,128)S(1)} all-gather(f32[1,2,64,64]{3,2,1,0:T(8,128)S(1)} %get-tuple-element.155), channel_id=1, replica_groups=mesh['chain'=8,'par'=4] {'par'}, dimensions={0}, use_global_device_ids=true | all-gather | bytes 163840 | tf_op jit(solution)/shard_map/all_gather | solution.py:119
  202.7 2.6 %fusion.4 = f32[4,2,4,32,64]{4,3,2,1,0:T(8,128)} fusion(f32[4,2,4,32,64]{3,4,2,1,0:T(8,128)S(1)} %bitcast.64, f32[4,2,64,64]{3,2,1,0:T(8,128)S(1)} %all_gather.11, f32[4,2,4,64]{3,2,1,0:T(4,128)S(1)} %bitcast.69), kind=kOutput, calls=%fused_computation.7 | convolution fusion | flops 50462720 | bytes 663552 | tf_op jit(solution)/shard_map/bsij,bstkj->bstki/dot_general | solution.py:69
  205.3 1.4 copy.138
  206.7 2.3 %reduce_sum.9 = f32[4,2,4,32,32]{3,4,2,1,0:T(8,128)} reduce(f32[4,2,4,32,32,2]{3,5,4,2,1,0:T(2,128)S(1)} %bitcast.65, f32[]{:T(128)} %constant.116.clone.1), dimensions={5}, to_apply=%region_6.7 | reduce | flops 32768 | bytes 393220 | tf_op jit(solution)/shard_map/reduce_sum | solution.py:76
  209.0 1.1 rev.6
  210.3 6.1 %reduce_window_sum.11 = f32[4,2,4,32,32]{4,3,2,1,0:T(8,128)S(1)} reduce-window(f32[4,2,4,32,32]{4,3,2,1,0:T(8,128)S(1)} %copy.139, f32[]{:T(128)} %constant.116.clone.1), window={size=1x1x1x1x32 pad=0_0x0_0x0_0x0_0x31_0}, to_apply=%region_7.8 | reduce-window | flops 1015808 | bytes 262148 | tf_op jit(solution)/shard_map/jit(cumsum)/reduce_window_sum | solution.py:78
  216.4 1.0 rev.7
  217.4 1.1 broadcast_multiply_fusion
  218.5 0.9 reshape.319
  (51 shorter events, 8.6 us)
Async XLA Ops:
  6.5 1.6 copy-start
  6.5 30.7 %all-gather.5.cloned.1.call-start = ((), (), s32[]{:S(2)}) async-start(), calls=%async_computation.2 | async-start | bytes 1179648 | tf_op jit(solution)/shard_map/all_gather | solution.py:11
  11.0 55.9 %all-gather.3.cloned.1.call-start = ((), (), s32[]{:S(2)}) async-start(), calls=%async_computation.1 | async-start | bytes 2359296 | tf_op jit(solution)/shard_map/all_gather | solution.py:11
  12.6 126.5 %all-reduce.3.cloned.1.call-start = ((), (), s32[]{:S(2)}) async-start(), calls=%async_computation.3 | async-start | bytes 786432 | tf_op jit(solution)/shard_map/psum | solution.py:26
  16.8 1.5 copy-start.5
  66.9 16.1 %copy-start.3 = (f32[1,16,2048]{2,1,0:T(8,128)S(1)}, f32[1,16,2048]{2,1,0:T(8,128)}, u32[]{:S(2)}) copy-start(f32[1,16,2048]{2,1,0:T(8,128)} %reshape.316) | copy-start | bytes 393220
  66.9 16.8 %copy-start.2 = (f32[1,16,4096]{2,1,0:T(8,128)S(1)}, f32[1,16,4096]{2,1,0:T(8,128)}, u32[]{:S(2)}) copy-start(f32[1,16,4096]{2,1,0:T(8,128)} %reshape.314) | copy-start | bytes 786436
  153.0 6.3 %copy-start.4 = (f32[64,64]{0,1:T(8,128)S(1)}, f32[64,64]{0,1:T(8,128)}, u32[]{:S(2)}) copy-start(f32[64,64]{0,1:T(8,128)} %copy.125) | copy-start | bytes 49156
  156.0 46.7 %copy-start.1 = (f32[4,2,4,32,32,2]{3,5,4,2,1,0:T(2,128)S(1)}, f32[4,2,4,32,32,2]{3,5,4,2,1,0:T(2,128)}, u32[]{:S(2)}) copy-start(f32[4,2,4,32,32,2]{3,5,4,2,1,0:T(2,128)} %copy.136) | copy-start | bytes 786436
  182.3 19.1 %all-to-all-start = ((f32[4,1,512]{2,1,0:T(1,128)}), f32[4,1,512]{2,1,0:T(1,128)S(1)}, u32[]{:S(2)}, u32[]{:S(2)}) async-start(f32[4,1,512]{2,1,0:T(1,128)} %reshape.325), calls=%async_computation | async-start | bytes 16384 | tf_op jit(solution)/shard_map/all_to_all | solution.py:120
Sparse Core Ops, SparseCore 0:
  11.1 26.0 all-gather.4
  39.1 27.7 all-gather.2
  84.6 54.4 all-reduce.2
where the time goes:
time: 227 us; the launch traced here: 226 us
  waiting for transfers between devices  103 us (45%)
  other arithmetic  55 us (24%)
  local copies, waits for them, and re-layouts  29.7 us (13%)
  blocking collectives  14.5 us (6%)
  between operations  13.3 us (6%)
  matrix products  5.48 us (2%)
  starting transfers between devices  4.62 us (2%)
    psum x1, waiting for transfers between devices, from_root(): return lax.psum(block, axis)  54.6 us
    all_gather x2, waiting for transfers between devices, prefix(): everything = jax.tree.map(lambda part: lax.all_gather(part, axis), x)  48.4 us
    select_n x16, other arithmetic, turn(): return jax.tree.map(lambda a, b: jnp.where(reached, a, b), new, before)  15.9 us
    all_gather x1, blocking collectives, local(): cholesky_triangle = lax.all_gather(lower_own, 'par', axis=0, tiled=True)  14.5 us
    another operation x4, other arithmetic, local(): lower_own = jnp.linalg.cholesky(assemble(same_part, cross_part, own_noise))  11.9 us
    another operation x3, other arithmetic, local(): rotated_own = jax.scipy.linalg.solve_triangular(lower_own, rhs, lower=True)  9.93 us
    reshape x2, local copies, waits for them, and re-layouts, assemble(): gram = whole.reshape(same_part.shape[:-2] + (order, order))  6.26 us
    another operation x1, other arithmetic, estimate_transmitted(): jnp.cumsum(squared_errors[..., ::-1], axis=-1)[..., ::-1] / terminal_number  6.14 us
  transfers between devices with their start and end apart: 4, of which 3 were waited for; matrix products, arithmetic and copies ran while one was open for 3% of the time, Pallas kernels for 0%

commit v1 on v0

--- a/solution.py
+++ b/solution.py
@@ -23,7 +23,7 @@
 
 def from_root(block, axis, owner):
     block = jnp.where(lax.axis_index(axis) == owner, block, jnp.zeros_like(block))
-    return lax.psum(block, axis)
+    return jnp.sum(lax.all_gather(block, axis), axis=0)
 
 
 def fold_stats(raw_gram, raw_cross):

time: 227 us -> 220 us (0.969)
  waiting for transfers between devices: 103 us -> 96.5 us
  local copies, waits for them, and re-layouts: 29.7 us -> 25.7 us
  other arithmetic: 55 us -> 58 us
    psum x1 -> x0, waiting for transfers between devices: 54.6 us -> none  [from_root(): return lax.psum(block, axis)]
    all_gather x0 -> x2, waiting for transfers between devices: none -> 43.1 us  [from_root(): return jnp.sum(lax.all_gather(block, axis), axis=0)]
    all_gather x2, waiting for transfers between devices: 48.4 us -> 53.3 us  [prefix(): everything = jax.tree.map(lambda part: lax.all_gather(part, axis), x)]
    reduce_sum x0 -> x2, other arithmetic: none -> 3.01 us  [from_root(): return jnp.sum(lax.all_gather(block, axis), axis=0)]
  transfers between devices with their start and end apart: 4 -> 5, of which waited for: 3 -> 4; matrix products, arithmetic and copies ran while one was open for 3% -> 6% of each run, Pallas kernels for 0% -> 0%
where the time goes in v1:
time: 220 us; the launch traced here: 219 us
  waiting for transfers between devices  96.5 us (44%)
  other arithmetic  58 us (26%)
  local copies, waits for them, and re-layouts  25.7 us (12%)
  blocking collectives  14.6 us (7%)
  between operations  13.4 us (6%)
  matrix products  5.48 us (2%)
  starting transfers between devices  4.73 us (2%)
    all_gather x2, waiting for transfers between devices, prefix(): everything = jax.tree.map(lambda part: lax.all_gather(part, axis), x)  53.3 us
    all_gather x2, waiting for transfers between devices, from_root(): return jnp.sum(lax.all_gather(block, axis), axis=0)  43.1 us
    select_n x16, other arithmetic, turn(): return jax.tree.map(lambda a, b: jnp.where(reached, a, b), new, before)  15.9 us
    all_gather x1, blocking collectives, local(): cholesky_triangle = lax.all_gather(lower_own, 'par', axis=0, tiled=True)  14.6 us
    another operation x4, other arithmetic, local(): lower_own = jnp.linalg.cholesky(assemble(same_part, cross_part, own_noise))  11.9 us
    another operation x3, other arithmetic, local(): rotated_own = jax.scipy.linalg.solve_triangular(lower_own, rhs, lower=True)  9.93 us
    reshape x2, local copies, waits for them, and re-layouts, assemble(): gram = whole.reshape(same_part.shape[:-2] + (order, order))  6.26 us
    another operation x1, other arithmetic, estimate_transmitted(): jnp.cumsum(squared_errors[..., ::-1], axis=-1)[..., ::-1] / terminal_number  6.14 us
  transfers between devices with their start and end apart: 5, of which 4 were waited for; matrix products, arithmetic and copies ran while one was open for 6% of the time, Pallas kernels for 0%

profile of v1, /device:TPU:0, one launch (start us, length us, event | category | flops | bytes accessed | tf_op | source)
XLA Modules:
  0.0 218.6 jit_solution(17466983416309041919)
XLA Ops:
  6.5 1.6 copy-done
  8.1 1.9 fusion
  10.0 0.9 all_gather_reshape.7
  11.7 0.9 all_gather_reshape.6
  13.6 23.6 %all-gather.9.cloned.1.call-done = f32[8,1,16,2048]{3,2,1,0:T(8,128)} async-done(((f32[1,1,16,2048]{3,2,1,0:T(8,128)}), f32[8,1,16,2048]{3,2,1,0:T(8,128)}) %all-gather.9.cloned.1.call-update) | async-done | bytes 1048592 | tf_op jit(solution)/shard_map/all_gather | solution.py:11
  37.2 29.7 %all-gather.7.cloned.1.call-done = f32[8,1,16,4096]{3,2,1,0:T(8,128)} async-done(((f32[1,1,16,4096]{3,2,1,0:T(8,128)}), f32[8,1,16,4096]{3,2,1,0:T(8,128)}) %all-gather.7.cloned.1.call-update) | async-done | bytes 2097168 | tf_op jit(solution)/shard_map/all_gather | solution.py:11
  66.9 16.1 %while.16 = (s32[]{:T(128)}, f32[1,16,4096]{2,1,0:T(8,128)S(1)}, f32[1,16,2048]{2,1,0:T(8,128)S(1)}, s32[]{:T(128)}, f32[8,1,16,4096]{3,2,1,0:T(8,128)}, /*index=5*/f32[8,1,16,2048]{3,2,1,0:T(8,128)}, s32[]{:T(128)}, s32[]{:T(128)}) while((s32[]{:T(128)}, f32[1,16,4096]{2,1,0:T(8,128)S(1)}, f32[1,16,2048]{2,1,0:T(8,128)S(1)}, ...), condition=%wide.region_1.2_spmd.clone, body=%wide.region_0.1_spmd.clone.sunk | while | flops 294916 | bytes 1179771 | solution.py:21
  66.9 1.0 add_select_fusion.9
  67.9 1.0 add_select_fusion.8
  68.9 0.9 add_select_fusion.9
  69.9 1.0 add_select_fusion.8
  71.0 0.9 add_select_fusion.9
  71.9 1.0 add_select_fusion.8
  73.0 0.9 add_select_fusion.9
  73.9 1.0 add_select_fusion.8
  75.0 0.9 add_select_fusion.9
  75.9 1.0 add_select_fusion.8
  77.0 0.9 add_select_fusion.9
  78.0 1.0 add_select_fusion.8
  79.0 0.9 add_select_fusion.9
  80.0 1.0 add_select_fusion.8
  81.0 0.9 add_select_fusion.9
  82.0 1.0 add_select_fusion.8
  85.8 1.3 copy.136
  87.3 20.0 %all-gather.13.cloned.1.call-done = f32[8,16,2048]{2,1,0:T(8,128)} async-done(((f32[1,16,2048]{2,1,0:T(8,128)}), f32[8,16,2048]{2,1,0:T(8,128)}) %all-gather.13.cloned.1.call-update) | async-done | bytes 1048592 | tf_op jit(solution)/shard_map/all_gather | solution.py:26
  107.3 1.3 reduce.12
  108.6 1.0 reshape_reshape.7
  109.6 1.3 slice_add_fusion.1
  110.9 1.3 copy.129
  112.3 1.3 copy.130
  113.7 23.1 %all-gather.11.cloned.1.call-done = f32[8,16,4096]{2,1,0:T(8,128)} async-done(((f32[1,16,4096]{2,1,0:T(8,128)}), f32[8,16,4096]{2,1,0:T(8,128)}) %all-gather.11.cloned.1.call-update) | async-done | bytes 2097168 | tf_op jit(solution)/shard_map/all_gather | solution.py:26
  136.8 1.7 reduce.11
  138.6 3.5 %reshape_reshape.6 = f32[1,2,32,2,32,2]{5,4,3,2,1,0:T(8,128)} reshape(f32[2,4096]{1,0:T(2,128)S(1)} %constant_dynamic-slice_fusion.1) | data formatting | bytes 65536 | tf_op jit(solution)/shard_map/reshape;reshape | solution.py:32
  142.1 3.4 %fusion.5 = (f32[2,32,32]{2,1,0:T(8,128)S(1)}, f32[2,32,32]{2,1,0:T(8,128)S(1)}) fusion(f32[1,2,32,2,32,2]{5,4,3,2,1,0:T(8,128)} %reshape_reshape.6), kind=kLoop, calls=%fused_computation.10 | loop fusion | flops 4096 | bytes 49152 | tf_op jit(solution)/shard_map/sub | solution.py:34
  145.6 3.0 %copy.146 = f32[1,2,32,2,32,2]{3,2,5,4,1,0:T(8,128)} copy(f32[1,2,32,2,32,2]{4,2,1,5,3,0:T(8,128)S(1)} %pad_maximum_fusion) | data formatting | bytes 65536 | tf_op jit(solution)/shard_map/reshape | solution.py:49
  148.5 3.3 %reshape.331 = f32[1,2,64,64]{2,3,1,0:T(8,128)S(1)} reshape(f32[1,2,32,2,32,2]{3,2,5,4,1,0:T(8,128)} %copy.146) | data formatting | bytes 65536 | tf_op jit(solution)/shard_map/reshape | solution.py:49
  152.1 11.7 %custom-call.8 = f32[1,2,64,64]{3,2,1,0:T(8,128)S(1)} custom-call(f32[1,2,64,64]{3,2,1,0:T(8,128)S(1)} %fusion.18), custom_call_target="Cholesky" | custom-call | tf_op jit(solution)/shard_map/jit(cholesky)/cholesky | solution.py:117
  164.1 9.8 %custom-call.9 = f32[2,1,64,64]{2,3,1,0:T(8,128)S(1)} custom-call(f32[2,1,64,64]{3,2,1,0:T(8,128)S(1)} %get-tuple-element.152), custom_call_target="InvertDiagBlocksLowerTriangular" | custom-call | tf_op jit(solution)/shard_map/jit(_solve_triangular)/vmap()/triangular_solve | solution.py:118
  174.9 4.6 %all-to-all-start = ((f32[4,1,512]{2,1,0:T(1,128)}), f32[4,1,512]{2,1,0:T(1,128)S(1)}, u32[]{:S(2)}, u32[]{:S(2)}) async-start(f32[4,1,512]{2,1,0:T(1,128)} %reshape.335), calls=%async_computation | async-start | bytes 16384 | tf_op jit(solution)/shard_map/all_to_all | solution.py:120
  179.5 14.6 %all_gather.27 = f32[4,2,64,64]{3,2,1,0:T(8,128)S(1)} all-gather(f32[1,2,64,64]{3,2,1,0:T(8,128)S(1)} %get-tuple-element.153), channel_id=1, replica_groups=mesh['chain'=8,'par'=4] {'par'}, dimensions={0}, use_global_device_ids=true | all-gather | bytes 163840 | tf_op jit(solution)/shard_map/all_gather | solution.py:119
  195.3 2.6 %fusion.4 = f32[4,2,4,32,64]{4,3,2,1,0:T(8,128)} fusion(f32[4,2,4,32,64]{3,4,2,1,0:T(8,128)S(1)} %bitcast.64, f32[4,2,64,64]{3,2,1,0:T(8,128)S(1)} %all_gather.27, f32[4,2,4,64]{3,2,1,0:T(4,128)S(1)} %bitcast.69), kind=kOutput, calls=%fused_computation.7 | convolution fusion | flops 50462720 | bytes 663552 | tf_op jit(solution)/shard_map/bsij,bstkj->bstki/dot_general | solution.py:69
  197.9 1.4 copy.138
  199.3 2.3 %reduce_sum.29 = f32[4,2,4,32,32]{3,4,2,1,0:T(8,128)} reduce(f32[4,2,4,32,32,2]{3,5,4,2,1,0:T(2,128)S(1)} %bitcast.65, f32[]{:T(128)} %constant.116.clone.1), dimensions={5}, to_apply=%region_6.7 | reduce | flops 32768 | bytes 393220 | tf_op jit(solution)/shard_map/reduce_sum | solution.py:76
  201.7 1.1 rev.6
  203.0 6.1 %reduce_window_sum.11 = f32[4,2,4,32,32]{4,3,2,1,0:T(8,128)S(1)} reduce-window(f32[4,2,4,32,32]{4,3,2,1,0:T(8,128)S(1)} %copy.139, f32[]{:T(128)} %constant.116.clone.1), window={size=1x1x1x1x32 pad=0_0x0_0x0_0x0_0x31_0}, to_apply=%region_7.8 | reduce-window | flops 1015808 | bytes 262148 | tf_op jit(solution)/shard_map/jit(cumsum)/reduce_window_sum | solution.py:78
  209.1 1.0 rev.7
  210.1 1.1 broadcast_multiply_fusion
  211.2 0.9 reshape.325
  (54 shorter events, 7.7 us)
Async XLA Ops:
  6.5 1.6 copy-start
  6.5 30.7 %all-gather.9.cloned.1.call-start = ((), (), s32[]{:S(2)}) async-start(), calls=%async_computation.2 | async-start | bytes 1179648 | tf_op jit(solution)/shard_map/all_gather | solution.py:11
  11.0 55.9 %all-gather.7.cloned.1.call-start = ((), (), s32[]{:S(2)}) async-start(), calls=%async_computation.1 | async-start | bytes 2359296 | tf_op jit(solution)/shard_map/all_gather | solution.py:11
  12.6 94.6 %all-gather.13.cloned.1.call-start = ((), (), s32[]{:S(2)}) async-start(), calls=%async_computation.4 | async-start | bytes 1179648 | tf_op jit(solution)/shard_map/all_gather | solution.py:26
  66.9 16.1 %copy-start.2 = (f32[1,16,2048]{2,1,0:T(8,128)S(1)}, f32[1,16,2048]{2,1,0:T(8,128)}, u32[]{:S(2)}) copy-start(f32[1,16,2048]{2,1,0:T(8,128)} %reshape.322) | copy-start | bytes 393220
  83.0 1.8 copy-start.3
  83.7 53.1 %all-gather.11.cloned.1.call-start = ((), (), s32[]{:S(2)}) async-start(), calls=%async_computation.3 | async-start | bytes 2359296 | tf_op jit(solution)/shard_map/all_gather | solution.py:26
  85.6 1.5 copy-start.4
  148.5 46.8 %copy-start.1 = (f32[4,2,4,32,32,2]{3,5,4,2,1,0:T(2,128)S(1)}, f32[4,2,4,32,32,2]{3,5,4,2,1,0:T(2,128)}, u32[]{:S(2)}) copy-start(f32[4,2,4,32,32,2]{3,5,4,2,1,0:T(2,128)} %copy.136) | copy-start | bytes 786436
  174.9 19.2 %all-to-all-start = ((f32[4,1,512]{2,1,0:T(1,128)}), f32[4,1,512]{2,1,0:T(1,128)S(1)}, u32[]{:S(2)}, u32[]{:S(2)}) async-start(f32[4,1,512]{2,1,0:T(1,128)} %reshape.335), calls=%async_computation | async-start | bytes 16384 | tf_op jit(solution)/shard_map/all_to_all | solution.py:120
Sparse Core Ops, SparseCore 0:
  11.1 26.0 all-gather.8
  39.1 27.7 all-gather.6
  83.9 23.3 all-gather.12
  109.0 27.7 all-gather.10
